TPU v7x, 512 devices: a whole 4x8x8 slice. The times are simulated.
512 devices in a mesh: cons: 16 (over y, x_lo), blk: 32 (over x_hi, z, core).
Axes of the slice: x: 4 (x_hi: 2, x_lo: 2; x = x_hi * 2 + x_lo), y: 8, z: 8, core: 2. Of those that a mesh axis runs over, the one named last changes fastest.
Arguments:
- elevation: bfloat16 [16, 1280, 6144], P('cons', 'blk'), may hold values from -6 to 6
- legendre: bfloat16 [1280, 768, 768], P('blk', 'cons'), may hold values from -5 to 5, as said below
- cycle_weight: float32 [1280], P('blk'), may hold values from 0.0001782951 to 0.0014263608
- love_factor: float32 [768], replicated, may hold values from 0.000390625 to 0.0052083335
- assignment: int32 [16], replicated, may hold values from 0 to 15, each once
Outputs:
- loading: float32 [16, 1280, 6144], P('cons', 'blk')
Inputs may be any that keep to these rules, and one draw needn't show every extreme that they name: `legendre`: fully normalized associated Legendre functions (the square integrates to 1 over [-1, 1]) of each cycle's latitude, every cycle within 26 degrees of the equator; zero where the degree is below the order.
All inputs are finite; a program needn't handle non-finite values.
Results may differ from a plain program's by a relative error of at most 0.02.
Values may be sent and summed in bfloat16 or wider, within the bound.
No kernel may reach another device: no remote copies, remote signals or barrier semaphores. Data moves between devices by JAX's collectives and lax.ppermute only.
A program may use at most 128 MiB of HBM per device.

v0:
```python
import jax
import jax.numpy as jnp
from jax import lax
from jax.sharding import Mesh
from jax.sharding import PartitionSpec as P

BLK = ("blk_0", "blk_1", "blk_2")


def filled_up(lines, length):
    spare = -lines.shape[0] % length
    if not spare:
        return lines
    return jnp.concatenate([lines, jnp.zeros((spare, *lines.shape[1:]), lines.dtype)])


def from_everyone(array, axis):
    copies = jnp.broadcast_to(array, (lax.axis_size(axis), *array.shape))
    return lax.all_to_all(copies, axis, split_axis=0, concat_axis=0, tiled=True)


def joined_along(tiles, dim):
    dims = list(tiles.shape[1:])
    dims[dim] *= tiles.shape[0]
    return jnp.moveaxis(tiles, 0, dim).reshape(dims)


def gathered_by_axis(array, axes, dim):
    far, near = axes
    tiles = from_everyone(from_everyone(array, far), near)
    return joined_along(tiles.swapaxes(0, 1).reshape(-1, *array.shape), dim)


def in_blocks(array, dim, length):
    dims = array.shape
    tiles = array.reshape(*dims[:dim], length, dims[dim] // length, *dims[dim + 1 :])
    return jnp.moveaxis(tiles, dim, 0)


def sent_and_summed(array, axis, dim):
    length = lax.axis_size(axis)
    tiles = lax.all_to_all(in_blocks(array, dim, length), axis, 0, 0, tiled=True)
    return jnp.sum(tiles.astype(jnp.float32), axis=0)


def summed_rows(array, axes, dim):
    far, near = axes
    tiles = in_blocks(array, dim, lax.axis_size(far))
    nearer = sent_and_summed(tiles, near, dim + 1)
    arrived = lax.all_to_all(
        nearer.astype(jnp.bfloat16), far, split_axis=0, concat_axis=0, tiled=True
    )
    return arrived.astype(jnp.float32).sum(axis=0)


def sum_by_parts(array, axes):
    lines = array.reshape(-1, array.shape[-1])
    padded = filled_up(lines, lax.axis_size(axes[0]) * lax.axis_size(axes[1]))
    whole = gathered_by_axis(summed_rows(padded, axes, 0).astype(jnp.bfloat16), axes, 0)
    return lax.slice_in_dim(whole, 0, len(lines)).reshape(array.shape).astype(jnp.float32)


def fourier_halves(offset, length, period, orders):
    lon_index = offset + jnp.arange(length, dtype=jnp.int32)
    order_index = jnp.arange(orders, dtype=jnp.int32)
    phases = lon_index[:, None] * order_index[None, :] % period
    angles = phases.astype(jnp.float32) * jnp.float32(2.0 * 3.141592653589793 / period)
    cosine = jnp.cos(angles).astype(jnp.bfloat16)
    minus_sine = (-jnp.sin(angles)).astype(jnp.bfloat16)
    return jnp.stack([cosine, minus_sine], axis=1)


def local(elevation, legendre, cycle_weight, love_factor, assignment):
    fld_dev, cycle_dev, longitudes = elevation.shape
    orders_dev = legendre.shape[1]
    orders = orders_dev * lax.axis_size("cons")
    quarter_len = longitudes // 4
    table = jnp.concatenate(
        [
            fourier_halves(quarter * quarter_len, quarter_len, longitudes, orders)
            for quarter in range(4)
        ],
        axis=0,
    )
    running = jnp.einsum("fjk,kpm->fjpm", elevation, table, preferred_element_type=jnp.float32)
    spectra = (running * cycle_weight[None, :, None, None]).astype(jnp.bfloat16)
    moved = lax.all_to_all(spectra, "cons", split_axis=3, concat_axis=0, tiled=True)
    fields = moved.shape[0]
    one_hot = (assignment[:, None] == jnp.arange(fields, dtype=jnp.int32)[None, :]).astype(
        jnp.bfloat16
    )
    ordered = jnp.einsum(
        "gf,fjpm->gjpm", one_hot, moved, preferred_element_type=jnp.float32
    ).astype(jnp.bfloat16)
    whole = sum_by_parts(
        jnp.einsum("jml,gjpm->lpgm", legendre, ordered, preferred_element_type=jnp.float32).astype(
            jnp.bfloat16
        ),
        (("blk_0", "blk_1"), "blk_2"),
    )
    coefficients = (whole * love_factor[:, None, None, None]).astype(jnp.bfloat16)
    order_index = lax.axis_index("cons") * orders_dev + jnp.arange(orders_dev, dtype=jnp.int32)
    order_factor = jnp.where(order_index == 0, 1.0, 2.0).astype(jnp.float32)
    summed = jnp.einsum(
        "jml,lpgm->gjpm", legendre, coefficients, preferred_element_type=jnp.float32
    )
    synthesis = (summed * order_factor[None, None, None, :]).astype(jnp.bfloat16)
    returned = lax.all_to_all(synthesis, "cons", split_axis=0, concat_axis=3, tiled=True)
    return jnp.einsum("fjpm,kpm->fjk", returned, table, preferred_element_type=jnp.float32)


def solution(mesh):
    torus = Mesh(
        mesh.devices.reshape(mesh.shape["cons"], 2, 8, 2), ("cons", "blk_0", "blk_1", "blk_2")
    )
    placed = (P("cons", BLK, None), P(BLK, "cons", None), P(BLK), P(), P())
    return jax.shard_map(
        local, mesh=torus, in_specs=placed, out_specs=P("cons", BLK, None), check_vma=False
    )
```

profile of v0, /device:TPU:1, one launch (start us, length us, event | category | flops | bytes accessed | tf_op | source)
XLA Modules:
  0.0 338.6 jit_solution(15464694889144117104)
XLA Ops:
  0.0 0.0 copy-start
  0.0 18.9 %cosine_convert_fusion.3 = bf16[1536,1,768]{2,0,1:T(8,128)(2,1)} fusion(), kind=kLoop, calls=%fused_computation.32 | loop fusion | flops 11796480 | bytes 2359296 | tf_op jit(solution)/shard_map/convert_element_type | solution.py:68
  19.0 40.5 %cosine_convert_fusion.2 = (bf16[1536,1,768]{2,0,1:T(8,128)(2,1)}, bf16[1536,1,768]{2,0,1:T(8,128)(2,1)}, bf16[1536,1,768]{2,0,1:T(8,128)(2,1)}) fusion(s32[1536]{0:T(1024)S(1)} %iota_add_fusion.2), kind=kLoop, calls=%fused_computation.27 | loop fusion | flops 27131904 | bytes 7084032 | tf_op jit(solution)/shard_map/convert_element_type | solution.py:68
  59.4 42.6 %cosine_convert_fusion = (bf16[1536,1,768]{2,0,1:T(8,128)(2,1)}, bf16[1536,1,768]{2,0,1:T(8,128)(2,1)}, bf16[1536,1,768]{2,0,1:T(8,128)(2,1)}, bf16[1536,1,768]{2,0,1:T(8,128)(2,1)}) fusion(s32[1536]{0:T(1024)S(1)} %iota_add_fusion, s32[1536]{0:T(1024)S(1)} %iota_add_fusion.1), kind=kLoop, calls=%fused_computation.17 | loop fusion | flops 28311552 | bytes 9449472 | tf_op jit(solution)/shard_map/convert_element_type | solution.py:68
  102.0 0.0 copy-start.1
  102.0 21.5 %maximum_maximum_fusion = bf16[6144,2,768]{2,0,1:T(8,128)(2,1)} fusion(bf16[1536,1,768]{2,0,1:T(8,128)(2,1)} %get-tuple-element.10, bf16[1536,1,768]{2,0,1:T(8,128)(2,1)} %get-tuple-element.9, bf16[1536,1,768]{2,0,1:T(8,128)(2,1)} %get-tuple-element.11, bf16[1536,1,768]{2,0,1:T(8,128)(2,1)} %get-tuple-element.12, bf16[1536,1,768]{2,0,1:T(8,128)(2,1)} %get-tuple-element.6, ...), kind=kLoop, calls=%fused_computation | loop fusion | flops 150994944 | bytes 37748736 | tf_op jit(solution)/shard_map/concatenate | solution.py:78
  123.5 0.0 copy-done.1
  123.5 0.0 copy-start.3
  123.6 9.6 %fusion.36 = bf16[1,40,2,768]{3,1,2,0:T(8,128)(2,1)S(1)} fusion(bf16[6144,2,768]{2,0,1:T(8,128)(2,1)} %maximum_maximum_fusion, bf16[1,40,6144]{2,1,0:T(8,128)(2,1)} %param.5, f32[40]{0:T(128)S(1)} %copy-done.1), kind=kOutput, calls=%fused_computation.51 | convolution fusion | flops 755097600 | bytes 19488928 | tf_op jit(solution)/shard_map/fjk,kpm->fjpm/dot_general | solution.py:85
  133.1 0.4 copy.22
  133.5 0.5 reshape.365
  134.1 17.0 %all_to_all.53 = bf16[16,2,1920]{2,1,0:T(2,128)(2,1)} all-to-all(bf16[16,2,1920]{2,1,0:T(2,128)(2,1)S(1)} %reshape.365), channel_id=1, replica_groups=mesh['cons'=16,'blk_0'=2,'blk_1'=8,'blk_2'=2] {'cons'}, dimensions={0} | all-to-all | bytes 245760 | tf_op jit(solution)/shard_map/all_to_all | solution.py:87
  151.1 1.5 reshape.366
  152.6 0.0 copy-done
  152.6 0.0 copy-done.3
  152.6 3.0 convert_bitcast_fusion.1
  155.6 12.0 %copy.26 = bf16[768,2,16,48]{3,2,1,0:T(8,128)(2,1)} copy(bf16[768,2,16,48]{0,2,1,3:T(8,128)(2,1)} %convert_bitcast_fusion.1) | data formatting | bytes 4718592 | tf_op jit(solution)/shard_map/convert_element_type | solution.py:96
  167.6 6.6 %copy.27 = bf16[2,16,768,48]{2,3,1,0:T(8,128)(2,1)} copy(bf16[2,16,768,48]{3,2,0,1:T(8,128)(2,1)} %bitcast.54) | data formatting | bytes 4718592 | tf_op jit(solution)/shard_map/transpose | solution.py:37
  174.2 11.5 %all_to_all.54 = bf16[2,16,768,48]{2,3,1,0:T(8,128)(2,1)} all-to-all(bf16[2,16,768,48]{2,3,1,0:T(8,128)(2,1)} %copy.27), channel_id=1, replica_groups=mesh['cons'=16,'blk_0'=2,'blk_1'=8,'blk_2'=2] {'blk_2'}, dimensions={0} | all-to-all | bytes 4718592 | tf_op jit(solution)/shard_map/all_to_all | solution.py:42
  185.7 3.4 %reduce_sum.24 = bf16[16,768,48]{1,2,0:T(8,128)(2,1)} reduce(bf16[2,16,768,48]{2,3,1,0:T(8,128)(2,1)} %all_to_all.54, bf16[]{:T(256)} %constant.40.clone.1), dimensions={0}, to_apply=%region_0.1 | reduce | flops 589824 | bytes 3538946 | tf_op jit(solution)/shard_map/reduce_sum | solution.py:43
  189.1 41.8 %all_to_all.55 = bf16[16,768,48]{1,2,0:T(8,128)(2,1)} all-to-all(bf16[16,768,48]{1,2,0:T(8,128)(2,1)} %reduce_sum.24), channel_id=1, replica_groups=mesh['cons'=16,'blk_0'=2,'blk_1'=8,'blk_2'=2] {'blk_0','blk_1'}, dimensions={0} | all-to-all | bytes 2359296 | tf_op jit(solution)/shard_map/all_to_all | solution.py:50
  230.9 1.4 reduce_sum.25
  232.4 1.1 broadcast_in_dim.10
  233.5 5.7 %all-to-all-start.3 = ((bf16[16,768,48]{1,2,0:T(8,128)(2,1)}), bf16[16,768,48]{1,2,0:T(8,128)(2,1)}, u32[]{:S(2)}, u32[]{:S(2)}) async-start(bf16[16,768,48]{1,2,0:T(8,128)(2,1)} %broadcast_in_dim.10), calls=%async_computation.3 | async-start | bytes 2359296 | tf_op jit(solution)/shard_map/all_to_all | solution.py:19
  239.2 28.6 %all-to-all-done.3 = bf16[16,768,48]{1,2,0:T(8,128)(2,1)} async-done(((bf16[16,768,48]{1,2,0:T(8,128)(2,1)}), bf16[16,768,48]{1,2,0:T(8,128)(2,1)}, u32[]{:S(2)}, u32[]{:S(2)}) %all-to-all-start.3) | async-done | bytes 1179680 | tf_op jit(solution)/shard_map/all_to_all | solution.py:19
  267.8 1.4 broadcast_in_dim.11
  269.3 8.1 %all_to_all.56 = bf16[2,16,768,48]{2,3,1,0:T(8,128)(2,1)S(1)} all-to-all(bf16[2,16,768,48]{2,3,1,0:T(8,128)(2,1)S(1)} %broadcast_in_dim.11), channel_id=1, replica_groups=mesh['cons'=16,'blk_0'=2,'blk_1'=8,'blk_2'=2] {'blk_2'}, dimensions={0} | all-to-all | bytes 4718592 | tf_op jit(solution)/shard_map/all_to_all | solution.py:19
  277.4 2.7 convert_bitcast_fusion
  280.1 0.0 copy-start.2
  280.1 9.2 %copy.28 = f32[16,2,768,48]{3,2,1,0:T(8,128)} copy(f32[16,2,768,48]{2,3,0,1:T(8,128)} %convert_bitcast_fusion) | data formatting | bytes 9437184 | tf_op jit(solution)/shard_map/convert_element_type | solution.py:60
  289.3 0.0 copy-done.2
  289.3 8.9 %multiply_convert_fusion = bf16[768,2,16,48]{3,2,1,0:T(8,128)(2,1)} fusion(f32[768,2,16,48]{3,2,1,0:T(8,128)} %bitcast.53, f32[768]{0:T(1024)S(1)} %copy-done.2), kind=kLoop, calls=%fused_computation.1 | loop fusion | flops 2359296 | bytes 7080960 | tf_op jit(solution)/shard_map/convert_element_type | solution.py:101
  298.2 10.0 %copy.29 = bf16[768,2,16,48]{0,2,1,3:T(8,128)(2,1)} copy(bf16[768,2,16,48]{3,2,1,0:T(8,128)(2,1)} %multiply_convert_fusion) | data formatting | bytes 4718592 | tf_op jit(solution)/shard_map/convert_element_type | solution.py:101
  308.2 3.6 %fusion.32 = bf16[16,40,2,48]{1,0,2,3:T(8,128)(2,1)} fusion(bf16[768,2,16,48]{0,2,1,3:T(8,128)(2,1)} %copy.29, bf16[40,48,768,1]{2,1,0,3:T(8,128)(2,1)S(1)} %bitcast.52, f32[48]{0:T(128)S(1)} %compare_select_fusion), kind=kOutput, calls=%fused_computation.48 | convolution fusion | flops 94494720 | bytes 5431488 | tf_op jit(solution)/shard_map/jml,lpgm->gjpm/dot_general | solution.py:104
  311.8 1.4 copy.31
  313.2 0.5 reshape.367
  313.7 11.3 %all_to_all.57 = bf16[16,2,1920]{2,1,0:T(2,128)(2,1)S(1)} all-to-all(bf16[16,2,1920]{2,1,0:T(2,128)(2,1)S(1)} %reshape.367), channel_id=1, replica_groups=mesh['cons'=16,'blk_0'=2,'blk_1'=8,'blk_2'=2] {'cons'}, dimensions={0} | all-to-all | bytes 245760 | tf_op jit(solution)/shard_map/all_to_all | solution.py:108
  324.9 0.4 reshape.368
  325.3 0.1 copy.32
  325.4 0.3 reshape.358
  325.7 12.9 %convolution_bitcast_fusion = f32[1,40,6144]{2,1,0:T(8,128)} fusion(bf16[40,2,768]{2,0,1:T(8,128)(2,1)S(1)} %reshape.358, bf16[6144,2,768]{2,0,1:T(8,128)(2,1)} %maximum_maximum_fusion), kind=kOutput, calls=%fused_computation.6 | convolution fusion | flops 754974720 | bytes 19980288 | tf_op jit(solution)/shard_map/fjpm,kpm->fjk/dot_general | solution.py:109
  (5 shorter events, 0.0 us)
Async XLA Ops:
  0.0 152.6 %copy-start = (bf16[40,48,768]{2,1,0:T(8,128)(2,1)S(1)}, bf16[40,48,768]{2,1,0:T(8,128)(2,1)}, u32[]{:S(2)}) copy-start(bf16[40,48,768]{2,1,0:T(8,128)(2,1)} %param.6) | copy-start | bytes 8847364
  102.0 21.5 %copy-start.1 = (f32[40]{0:T(128)S(1)}, f32[40]{0:T(128)}, u32[]{:S(2)}) copy-start(f32[40]{0:T(128)} %param.7) | copy-start | bytes 484
  123.5 29.0 %copy-start.3 = (s32[16]{0:T(128)S(1)}, s32[16]{0:T(128)}, u32[]{:S(2)}) copy-start(s32[16]{0:T(128)} %param.9) | copy-start | bytes 196
  233.5 34.3 %all-to-all-start.3 = ((bf16[16,768,48]{1,2,0:T(8,128)(2,1)}), bf16[16,768,48]{1,2,0:T(8,128)(2,1)}, u32[]{:S(2)}, u32[]{:S(2)}) async-start(bf16[16,768,48]{1,2,0:T(8,128)(2,1)} %broadcast_in_dim.10), calls=%async_computation.3 | async-start | bytes 2359296 | tf_op jit(solution)/shard_map/all_to_all | solution.py:19
  280.1 9.2 %copy-start.2 = (f32[768]{0:T(1024)S(1)}, f32[768]{0:T(1024)}, u32[]{:S(2)}) copy-start(f32[768]{0:T(1024)} %param.8) | copy-start | bytes 9220
where the time goes:
time: 340 us; the launch traced here: 339 us
  other arithmetic  140 us (41%)
  blocking collectives  89.6 us (26%)
  local copies, waits for them, and re-layouts  45.6 us (13%)
  matrix products  29 us (9%)
  waiting for transfers between devices  28.6 us (8%)
  starting transfers between devices  5.71 us (2%)
    convert_element_type x3, other arithmetic, fourier_halves(): cosine = jnp.cos(angles).astype(jnp.bfloat16)  102 us
    all_to_all x1, blocking collectives, summed_rows(): lax.all_to_all(nearer.astype(jnp.bfloat16), far, split_axis=0, concat_axi...  41.8 us
    all_to_all x1, waiting for transfers between devices, from_everyone(): return lax.all_to_all(copies, axis, split_axis=0, concat_axis=0, tiled=True)  28.6 us
    concatenate x1, other arithmetic, local(): jnp.concatenate([fourier_halves(quarter * quarter_len, quarter_len, longi...  21.5 us
    all_to_all x1, blocking collectives, local(): lax.all_to_all(spectra, 'cons', split_axis=3, concat_axis=0, tiled=True)  17 us
    dot_general x1, matrix products, local(): jnp.einsum('fjpm,kpm->fjk', returned, table, preferred_element_type=jnp.f...  12.9 us
    convert_element_type x1, local copies, waits for them, and re-layouts, local(): jnp.einsum('jml,gjpm->lpgm', legendre, ordered, preferred_element_type=jn...  12 us
    all_to_all x1, blocking collectives, sent_and_summed(): lax.all_to_all(in_blocks(array, dim, length), axis, 0, 0, tiled=True)  11.5 us
  transfers between devices with their start and end apart: 1, of which 1 were waited for; matrix products, arithmetic and copies ran while one was open for 0% of the time, Pallas kernels for 0%

commit v1 on v0

v1 whole, which is shorter than its diff:
```python
import functools

import jax
import jax.numpy as jnp
import numpy as np
from jax import lax
from jax.experimental import pallas as pl
from jax.experimental.pallas import tpu as pltpu
from jax.sharding import Mesh
from jax.sharding import PartitionSpec as P

BLK = ("blk_0", "blk_1", "blk_2")
FAR = ("blk_0", "blk_1")
TEAM = ("cons", "blk_2")
FINE = 16
INNER = FINE * FINE


def angle_tables(steps, stride, period, orders):
    phases = (np.arange(steps)[:, None] * stride * np.arange(orders)[None, :]) % period
    angles = phases * (2.0 * np.pi / period)
    return np.stack([np.cos(angles), np.sin(angles)]).astype(np.float32)


def inner_table(coarse_ref, fine_ref, table_ref, lanes):
    fine_cos, fine_sin = fine_ref[0, :, lanes], fine_ref[1, :, lanes]
    for step in range(FINE):
        rows = slice(step * FINE, (step + 1) * FINE)
        coarse_cos = coarse_ref[0, step : step + 1, lanes]
        coarse_sin = coarse_ref[1, step : step + 1, lanes]
        cosine = coarse_cos * fine_cos - coarse_sin * fine_sin
        sine = coarse_sin * fine_cos + coarse_cos * fine_sin
        table_ref[0, rows, lanes] = cosine.astype(jnp.bfloat16)
        table_ref[1, rows, lanes] = (-sine).astype(jnp.bfloat16)


def forward_kernel(
    elevation_ref, weight_ref, coarse_ref, fine_ref, turn_ref, out_ref, rows_ref, table_ref
):
    cycles = elevation_ref.shape[0]
    turns = turn_ref.shape[1]

    @pl.when(pl.program_id(0) == 0)
    def _():
        for turn in range(turns):
            rows_ref[turn * cycles : (turn + 1) * cycles, :] = elevation_ref[
                :, turn * INNER : (turn + 1) * INNER
            ]

    lanes = slice(None)
    inner_table(coarse_ref, fine_ref, table_ref, lanes)
    even = jnp.dot(rows_ref[...], table_ref[0], preferred_element_type=jnp.float32)
    odd = jnp.dot(rows_ref[...], table_ref[1], preferred_element_type=jnp.float32)
    first = second = None
    for turn in range(turns):
        rows = slice(turn * cycles, (turn + 1) * cycles)
        cosine, sine = turn_ref[0, turn : turn + 1, :], turn_ref[1, turn : turn + 1, :]
        one = even[rows] * cosine + odd[rows] * sine
        two = odd[rows] * cosine - even[rows] * sine
        first = one if first is None else first + one
        second = two if second is None else second + two
    weight = weight_ref[...]
    out_ref[0] = (first * weight).astype(jnp.bfloat16)
    out_ref[1] = (second * weight).astype(jnp.bfloat16)


def forward(elevation, weight, coarse, fine, turn):
    cycles, longitudes = elevation.shape
    orders = coarse.shape[2]
    turns = longitudes // INNER
    width = 256
    whole = lambda m: (0, 0)
    part = lambda m: (0, 0, m)
    return pl.pallas_call(
        forward_kernel,
        grid=(orders // width,),
        in_specs=[
            pl.BlockSpec((cycles, longitudes), whole),
            pl.BlockSpec((cycles, 1), whole),
            pl.BlockSpec((2, FINE, width), part),
            pl.BlockSpec((2, FINE, width), part),
            pl.BlockSpec((2, turns, width), part),
        ],
        out_specs=pl.BlockSpec((2, cycles, width), part),
        out_shape=jax.ShapeDtypeStruct((2, cycles, orders), jnp.bfloat16),
        scratch_shapes=[
            pltpu.VMEM((turns * cycles, INNER), jnp.bfloat16),
            pltpu.VMEM((2, INNER, width), jnp.bfloat16),
        ],
        cost_estimate=pl.CostEstimate(
            flops=4 * cycles * longitudes * orders, bytes_accessed=1 << 20, transcendentals=0
        ),
        name="forward_dft",
    )(elevation, weight, coarse, fine, turn)


def inverse_kernel(
    synthesis_ref, coarse_ref, fine_ref, turn_ref, out_ref, rows_ref, table_ref
):
    cycles = synthesis_ref.shape[1]
    count = out_ref.shape[1] // INNER

    @pl.when(pl.program_id(0) == 0)
    def _():
        inner_table(coarse_ref, fine_ref, table_ref, slice(None))

    first = synthesis_ref[0].astype(jnp.float32)
    second = synthesis_ref[1].astype(jnp.float32)
    base = pl.program_id(0) * count
    for step in range(count):
        rows = slice(step * cycles, (step + 1) * cycles)
        cosine = turn_ref[0, pl.ds(base + step, 1), :]
        sine = turn_ref[1, pl.ds(base + step, 1), :]
        rows_ref[0, rows, :] = (first * cosine - second * sine).astype(jnp.bfloat16)
        rows_ref[1, rows, :] = (first * sine + second * cosine).astype(jnp.bfloat16)
    dims = (((1,), (1,)), ((), ()))
    result = lax.dot_general(
        rows_ref[0], table_ref[0], dims, preferred_element_type=jnp.float32
    ) + lax.dot_general(rows_ref[1], table_ref[1], dims, preferred_element_type=jnp.float32)
    for step in range(count):
        out_ref[:, step * INNER : (step + 1) * INNER] = result[
            step * cycles : (step + 1) * cycles
        ]


def inverse(synthesis, coarse, fine, turn, longitudes):
    _, cycles, orders = synthesis.shape
    turns = longitudes // INNER
    count = 6
    whole = lambda a: (0, 0, 0)
    return pl.pallas_call(
        inverse_kernel,
        grid=(turns // count,),
        in_specs=[
            pl.BlockSpec((2, cycles, orders), whole),
            pl.BlockSpec((2, FINE, orders), whole),
            pl.BlockSpec((2, FINE, orders), whole),
            pl.BlockSpec((2, turns, orders), whole),
        ],
        out_specs=pl.BlockSpec((cycles, count * INNER), lambda a: (0, a)),
        out_shape=jax.ShapeDtypeStruct((cycles, longitudes), jnp.float32),
        scratch_shapes=[
            pltpu.VMEM((2, count * cycles, orders), jnp.bfloat16),
            pltpu.VMEM((2, INNER, orders), jnp.bfloat16),
        ],
        cost_estimate=pl.CostEstimate(
            flops=4 * cycles * longitudes * orders, bytes_accessed=1 << 20, transcendentals=0
        ),
        name="inverse_dft",
    )(synthesis, coarse, fine, turn)


def local(elevation, legendre, cycle_weight, love_factor, assignment):
    fld_dev, cycle_dev, longitudes = elevation.shape
    orders_dev, degrees = legendre.shape[1:]
    groups = lax.axis_size("cons")
    cores = lax.axis_size("blk_2")
    far = lax.axis_size("blk_0") * lax.axis_size("blk_1")
    orders = orders_dev * groups
    half = orders_dev // cores
    core = lax.axis_index("blk_2")
    coarse = jnp.asarray(angle_tables(FINE, FINE, longitudes, orders))
    fine = jnp.asarray(angle_tables(FINE, 1, longitudes, orders))
    turn = jnp.asarray(angle_tables(longitudes // INNER, INNER, longitudes, orders))

    def half_of(index):
        return lax.dynamic_slice_in_dim(legendre, index * half, half, 1)

    swapped = lax.ppermute(half_of(1 - core), "blk_2", [(0, 1), (1, 0)])
    own = half_of(core)
    is_first = core == 0
    values = jnp.stack(
        [jnp.where(is_first, own, swapped), jnp.where(is_first, swapped, own)], axis=0
    )

    spectra = forward(elevation[0], cycle_weight[:, None], coarse, fine, turn)
    outgoing = spectra.reshape(2, cycle_dev, groups * cores, half)
    outgoing = outgoing.transpose(2, 0, 1, 3).reshape(groups * cores, -1)
    moved = lax.all_to_all(outgoing, TEAM, 0, 0, tiled=True)
    moved = moved.reshape(groups, cores, 2, cycle_dev, half)
    one_hot = (
        assignment[:, None] == jnp.arange(groups, dtype=jnp.int32)[None, :]
    ).astype(jnp.bfloat16)
    ordered = jnp.einsum(
        "gf,fspjm->gspjm", one_hot, moved, preferred_element_type=jnp.float32
    ).astype(jnp.bfloat16)
    partial = jnp.einsum(
        "sjml,gspjm->mpgl", values, ordered, preferred_element_type=jnp.float32
    ).astype(jnp.bfloat16)
    lines = half * 2 * groups
    arrived = lax.all_to_all(
        partial.reshape(far, lines // far, degrees), FAR, 0, 0, tiled=True
    )
    analysis = jnp.sum(arrived.astype(jnp.float32), axis=0)
    scaled = (analysis * love_factor[None, :]).astype(jnp.bfloat16)
    copies = jnp.broadcast_to(scaled[None], (far, lines // far, degrees))
    coefficients = lax.all_to_all(copies, FAR, 0, 0, tiled=True)
    coefficients = coefficients.reshape(half, 2, groups, degrees)
    summed = jnp.einsum(
        "sjml,mpgl->gspjm", values, coefficients, preferred_element_type=jnp.float32
    )
    order_index = lax.axis_index("cons") * orders_dev + core * half + jnp.arange(half)
    order_factor = jnp.where(order_index == 0, 1.0, 2.0).astype(jnp.float32)
    synthesis = (summed * order_factor).astype(jnp.bfloat16)
    returned = lax.all_to_all(
        synthesis.reshape(groups * cores, -1), TEAM, 0, 0, tiled=True
    )
    returned = returned.reshape(groups * cores, 2, cycle_dev, half)
    returned = returned.transpose(1, 2, 0, 3).reshape(2, cycle_dev, orders)
    return inverse(returned, coarse, fine, turn, longitudes)[None]


def solution(mesh):
    torus = Mesh(
        mesh.devices.reshape(mesh.shape["cons"], 2, 8, 2), ("cons", "blk_0", "blk_1", "blk_2")
    )
    placed = (P("cons", BLK, None), P(BLK, "cons", None), P(BLK), P(), P())
    return jax.shard_map(
        local, mesh=torus, in_specs=placed, out_specs=P("cons", BLK, None), check_vma=False
    )
```

time: 340 us -> 148 us (0.44)
  other arithmetic: 140 us -> 7.09 us
  blocking collectives: 89.6 us -> 56.8 us
  local copies, waits for them, and re-layouts: 45.6 us -> 14.3 us
  matrix products: 29 us -> 5.51 us
  starting transfers between devices: 5.71 us -> 18.3 us
  waiting for transfers between devices: 28.6 us -> 37.9 us
  Pallas kernels: 0 us -> 7.53 us
    convert_element_type x5 -> x1, other arithmetic: 114 us -> 0.01 us  [local(): scaled = (analysis * love_factor[None, :]).astype(jnp.bfloat16)]
    all_to_all x5 -> x2, blocking collectives: 89.6 us -> 56.8 us  [the longest x1 41.3 us: local(): lax.all_to_all(partial.reshape(far, lines // far, degrees), FAR, 0, 0, ti...]
    convert_element_type x5 -> x1, local copies, waits for them, and re-layouts: 33.1 us -> 0.57 us  [local(): synthesis = (summed * order_factor).astype(jnp.bfloat16)]
    dot_general x4 -> x2, matrix products: 29 us -> 5.51 us  [the longest x1 3.32 us: local(): jnp.einsum('sjml,mpgl->gspjm', values, coefficients, preferred_element_ty...]
    concatenate x1 -> x0, other arithmetic: 21.5 us -> none  [local(): jnp.concatenate([fourier_halves(quarter * quarter_len, quarter_len, longi...]
    all_to_all x1 -> x2, waiting for transfers between devices: 28.6 us -> 37.8 us  [the longest x1 28.5 us: local(): coefficients = lax.all_to_all(copies, FAR, 0, 0, tiled=True)]
    ppermute x0 -> x1, starting transfers between devices: none -> 8.74 us  [local(): swapped = lax.ppermute(half_of(1 - core), 'blk_2', [(0, 1), (1, 0)])]
    pallas_call x0 -> x2, Pallas kernels: none -> 7.53 us  [the longest x1 3.96 us: inverse(): pl.pallas_call(inverse_kernel, grid=(turns // count,), in_specs=[pl.Block...]
  transfers between devices with their start and end apart: 1 -> 3, of which waited for: 1 -> 2; matrix products, arithmetic and copies ran while one was open for 0% -> 5% of each run, Pallas kernels for 0% -> 2%
where the time goes in v1:
time: 148 us
  blocking collectives  56.8 us (38%)
  waiting for transfers between devices  37.9 us (26%)
  starting transfers between devices  18.3 us (12%)
  local copies, waits for them, and re-layouts  14.3 us (10%)
  Pallas kernels  7.53 us (5%)
  other arithmetic  7.09 us (5%)
  matrix products  5.51 us (4%)
    all_to_all x1, blocking collectives, local(): lax.all_to_all(partial.reshape(far, lines // far, degrees), FAR, 0, 0, ti...  41.3 us
    all_to_all x1, waiting for transfers between devices, local(): coefficients = lax.all_to_all(copies, FAR, 0, 0, tiled=True)  28.5 us
    all_to_all x1, blocking collectives, local(): lax.all_to_all(synthesis.reshape(groups * cores, -1), TEAM, 0, 0, tiled=T...  15.5 us
    all_to_all x1, waiting for transfers between devices, local(): moved = lax.all_to_all(outgoing, TEAM, 0, 0, tiled=True)  9.3 us
    ppermute x1, starting transfers between devices, local(): swapped = lax.ppermute(half_of(1 - core), 'blk_2', [(0, 1), (1, 0)])  8.74 us
    all_to_all x1, starting transfers between devices, local(): coefficients = lax.all_to_all(copies, FAR, 0, 0, tiled=True)  5.88 us
    pallas_call x1, Pallas kernels, inverse(): pl.pallas_call(inverse_kernel, grid=(turns // count,), in_specs=[pl.Block...  3.96 us
    all_to_all x1, starting transfers between devices, local(): moved = lax.all_to_all(outgoing, TEAM, 0, 0, tiled=True)  3.65 us
  transfers between devices with their start and end apart: 3, of which 2 were waited for; matrix products, arithmetic and copies ran while one was open for 5% of the time, Pallas kernels for 2%

profile of v1, /device:TPU:1, one launch (start us, length us, event | category | flops | bytes accessed | tf_op | source)
XLA Modules:
  0.0 147.6 jit_solution(16901714720530248306)
XLA Ops:
  0.0 2.0 %constant_dynamic-slice_fusion.1 = (bf16[40,24,768]{2,1,0:T(8,128)(2,1)S(1)}, bf16[40,24,768]{2,1,0:T(8,128)(2,1)S(1)}) fusion(bf16[40,48,768]{2,1,0:T(8,128)(2,1)} %param.9, s32[]{:T(128)S(6)} %select_n.27, s32[]{:T(128)S(6)} %select_n.28), kind=kLoop, calls=%fused_computation.17 | loop fusion | bytes 5898248 | tf_op jit(solution)/shard_map/dynamic_slice | solution.py:167
  2.0 0.0 copy-start.2
  2.0 1.4 copy.38
  3.4 8.7 %collective-permute-start = (bf16[40,24,768]{2,0,1:T(8,128)(2,1)}, bf16[40,24,768]{2,0,1:T(8,128)(2,1)}, u32[]{:S(2)}, u32[]{:S(2)}) collective-permute-start(bf16[40,24,768]{2,0,1:T(8,128)(2,1)} %copy.38), channel_id=1, source_target_pairs={{0,1},{1,0},{2,3},{3,2},{4,5},{5,4},{6,7},{7,6},{8,9},{9,8},{10,11... | collective-permute-start | bytes 4423688 | tf_op jit(solution)/shard_map/ppermute | solution.py:169
  12.2 0.0 copy-done.2
  12.2 0.7 copy.22.weight_ref
  12.9 3.6 %forward_dft.1 = bf16[2,40,768]{2,1,0:T(8,128)(2,1)} custom-call(bf16[40,6144]{1,0:T(8,128)(2,1)} %bitcast.56, f32[40,1]{1,0:T(8,128)} %copy.22.weight_ref, f32[2,16,768]{2,1,0:T(8,128)} %constant.31.clone.coarse_ref, f32[2,16,768]{2,1,0:T(8,128)} %constant.32.clone.fine_ref, f32[2,24,768]{2,1,0:T(8,128)} %constant.33.clone.turn_ref), custom_call_target="tpu_custom_call" | custom-call | flops 754974720 | bytes 1048576 | tf_op jit(solution)/shard_map/forward_dft/pallas_call | solution.py:74
  16.4 1.1 copy.23
  17.5 0.3 copy.24
  17.9 0.8 all_to_all.24
  18.7 0.6 broadcast.37
  19.3 1.3 reduce.2
  20.6 0.8 reshape.66
  21.4 3.6 %all-to-all-start = ((bf16[32,2,960]{2,1,0:T(2,128)(2,1)}), bf16[32,2,960]{2,1,0:T(2,128)(2,1)S(1)}, u32[]{:S(2)}, u32[]{:S(2)}) async-start(bf16[32,2,960]{2,1,0:T(2,128)(2,1)} %reshape.66), calls=%async_computation | async-start | bytes 262144 | tf_op jit(solution)/shard_map/all_to_all | solution.py:179
  25.1 9.3 %all-to-all-done = bf16[32,2,960]{2,1,0:T(2,128)(2,1)S(1)} async-done(((bf16[32,2,960]{2,1,0:T(2,128)(2,1)}), bf16[32,2,960]{2,1,0:T(2,128)(2,1)S(1)}, u32[]{:S(2)}, u32[]{:S(2)}) %all-to-all-start) | async-done | bytes 122912 | tf_op jit(solution)/shard_map/all_to_all | solution.py:179
  34.4 0.2 reshape.67
  34.6 0.7 reduce
  35.3 0.9 reshape.55
  36.2 0.7 copy.26
  36.9 0.0 collective-permute-done
  36.9 0.0 copy-start.3
  36.9 2.8 %select_bitcast_fusion.1 = (bf16[1,40,24,768]{3,1,0,2:T(8,128)(2,1)S(1)}, bf16[1,40,24,768]{3,1,0,2:T(8,128)(2,1)}) fusion(bf16[40,24,768]{2,0,1:T(8,128)(2,1)} %collective-permute-done, pred[]{:T(512)S(6)} %eq.26, bf16[40,24,768]{2,1,0:T(8,128)(2,1)S(1)} %get-tuple-element.7), kind=kLoop, calls=%fused_computation.6 | loop fusion | flops 1474560 | bytes 5898241 | tf_op jit(solution)/shard_map/stack | solution.py:172
  39.8 0.0 copy-done.3
  39.8 2.2 %bitcast_convert_fusion = bf16[24,16,2,768]{3,1,2,0:T(8,128)(2,1)S(1)} fusion(bf16[1,40,24,768]{3,1,0,2:T(8,128)(2,1)} %get-tuple-element.6, bf16[1,40,24,768]{3,1,0,2:T(8,128)(2,1)S(1)} %get-tuple-element.5, bf16[16,2,2,40,24]{3,0,1,2,4:T(8,128)(2,1)S(1)} %copy.26, s32[16]{0:T(128)S(1)} %copy-done.3), kind=kOutput, calls=%fused_computation.1 | convolution fusion | flops 98464000 | bytes 4251712 | tf_op jit(solution)/shard_map/sjml,gspjm->mpgl/dot_general | solution.py:187
  42.0 0.0 copy-start.1
  42.0 41.3 %all_to_all.30 = bf16[16,48,768]{2,1,0:T(8,128)(2,1)S(1)} all-to-all(bf16[16,48,768]{2,1,0:T(8,128)(2,1)S(1)} %bitcast.54), channel_id=1, replica_groups=mesh['cons'=16,'blk_0'=2,'blk_1'=8,'blk_2'=2] {'blk_0','blk_1'}, dimensions={0} | all-to-all | bytes 2359296 | tf_op jit(solution)/shard_map/all_to_all | solution.py:191
  83.3 0.2 convert_reduce_fusion
  83.4 0.0 copy-done.1
  83.5 1.1 broadcast_in_dim.25
  84.6 0.0 copy-start
  84.6 5.9 %all-to-all-start.2 = ((bf16[16,48,768]{2,1,0:T(8,128)(2,1)}), bf16[16,48,768]{2,1,0:T(8,128)(2,1)}, u32[]{:S(2)}, u32[]{:S(2)}) async-start(bf16[16,48,768]{2,1,0:T(8,128)(2,1)} %broadcast_in_dim.25), calls=%async_computation.2 | async-start | bytes 2359296 | tf_op jit(solution)/shard_map/all_to_all | solution.py:197
  90.5 28.5 %all-to-all-done.2 = bf16[16,48,768]{2,1,0:T(8,128)(2,1)} async-done(((bf16[16,48,768]{2,1,0:T(8,128)(2,1)}), bf16[16,48,768]{2,1,0:T(8,128)(2,1)}, u32[]{:S(2)}, u32[]{:S(2)}) %all-to-all-start.2) | async-done | bytes 1179680 | tf_op jit(solution)/shard_map/all_to_all | solution.py:197
  119.0 0.0 copy-done
  119.0 3.3 %fusion.4 = bf16[16,2,2,40,24]{3,0,1,2,4:T(8,128)(2,1)S(1)} fusion(bf16[24,2,16,768,1]{3,2,4,1,0:T(8,128)(2,1)} %bitcast.16, bf16[1,40,24,768]{3,1,0,2:T(8,128)(2,1)S(1)} %copy-done, bf16[1,40,24,768]{3,1,0,2:T(8,128)(2,1)S(1)} %get-tuple-element.5, f32[24]{0:T(128)S(1)} %compare_select_fusion), kind=kOutput, calls=%fused_computation.10 | convolution fusion | flops 100392960 | bytes 4251744 | tf_op jit(solution)/shard_map/sjml,mpgl->gspjm/dot_general | solution.py:199
  122.3 0.6 copy.30
  122.9 0.8 all_to_all.25
  123.7 1.3 reduce.3
  125.1 0.2 reshape.68
  125.3 15.5 %all_to_all.31 = bf16[32,2,960]{2,1,0:T(2,128)(2,1)S(1)} all-to-all(bf16[32,2,960]{2,1,0:T(2,128)(2,1)S(1)} %reshape.68), channel_id=1, replica_groups=mesh['cons'=16,'blk_0'=2,'blk_1'=8,'blk_2'=2] {'cons','blk_2'}, dimensions={0} | all-to-all | bytes 245760 | tf_op jit(solution)/shard_map/all_to_all | solution.py:205
  140.8 0.2 reshape.69
  140.9 0.7 reduce.1
  141.6 0.9 reshape.58
  142.5 0.3 copy.32
  142.8 0.8 copy.33.synthesis_ref
  143.6 4.0 %inverse_dft.1 = f32[40,6144]{1,0:T(8,128)} custom-call(bf16[2,40,768]{2,1,0:T(8,128)(2,1)} %copy.33.synthesis_ref, f32[2,16,768]{2,1,0:T(8,128)} %constant.31.clone.coarse_ref, f32[2,16,768]{2,1,0:T(8,128)} %constant.32.clone.fine_ref, f32[2,24,768]{2,1,0:T(8,128)} %constant.33.clone.turn_ref), custom_call_target="tpu_custom_call" | custom-call | flops 754974720 | bytes 1048576 | tf_op jit(solution)/shard_map/inverse_dft/pallas_call | solution.py:131
  (2 shorter events, 0.0 us)
Async XLA Ops:
  2.0 10.1 %copy-start.2 = (f32[40]{0:T(128)S(1)}, f32[40]{0:T(128)}, u32[]{:S(2)}) copy-start(f32[40]{0:T(128)} %param.10) | copy-start | bytes 484
  3.4 33.5 %collective-permute-start = (bf16[40,24,768]{2,0,1:T(8,128)(2,1)}, bf16[40,24,768]{2,0,1:T(8,128)(2,1)}, u32[]{:S(2)}, u32[]{:S(2)}) collective-permute-start(bf16[40,24,768]{2,0,1:T(8,128)(2,1)} %copy.38), channel_id=1, source_target_pairs={{0,1},{1,0},{2,3},{3,2},{4,5},{5,4},{6,7},{7,6},{8,9},{9,8},{10,11... | collective-permute-start | bytes 4423688 | tf_op jit(solution)/shard_map/ppermute | solution.py:169
  21.4 13.0 %all-to-all-start = ((bf16[32,2,960]{2,1,0:T(2,128)(2,1)}), bf16[32,2,960]{2,1,0:T(2,128)(2,1)S(1)}, u32[]{:S(2)}, u32[]{:S(2)}) async-start(bf16[32,2,960]{2,1,0:T(2,128)(2,1)} %reshape.66), calls=%async_computation | async-start | bytes 262144 | tf_op jit(solution)/shard_map/all_to_all | solution.py:179
  36.9 2.8 %copy-start.3 = (s32[16]{0:T(128)S(1)}, s32[16]{0:T(128)}, u32[]{:S(2)}) copy-start(s32[16]{0:T(128)} %param.12) | copy-start | bytes 196
  42.0 41.5 %copy-start.1 = (f32[768]{0:T(1024)S(1)}, f32[768]{0:T(1024)}, u32[]{:S(2)}) copy-start(f32[768]{0:T(1024)} %param.11) | copy-start | bytes 9220
  84.6 34.5 %copy-start = (bf16[1,40,24,768]{3,1,0,2:T(8,128)(2,1)S(1)}, bf16[1,40,24,768]{3,1,0,2:T(8,128)(2,1)}, u32[]{:S(2)}) copy-start(bf16[1,40,24,768]{3,1,0,2:T(8,128)(2,1)} %get-tuple-element.6) | copy-start | bytes 4423684
  84.6 34.5 %all-to-all-start.2 = ((bf16[16,48,768]{2,1,0:T(8,128)(2,1)}), bf16[16,48,768]{2,1,0:T(8,128)(2,1)}, u32[]{:S(2)}, u32[]{:S(2)}) async-start(bf16[16,48,768]{2,1,0:T(8,128)(2,1)} %broadcast_in_dim.25), calls=%async_computation.2 | async-start | bytes 2359296 | tf_op jit(solution)/shard_map/all_to_all | solution.py:197
